TPU v7x, 256 devices: a whole 4x4x8 slice. The times are simulated.
256 devices in a mesh: gx: 2 (over z_lo), gy: 16 (over x, y), gz: 8 (over z_hi, core).
Axes of the slice: x: 4, y: 4, z: 8 (z_hi: 4, z_lo: 2; z = z_hi * 2 + z_lo), core: 2. Of those that a mesh axis runs over, the one named last changes fastest.
Arguments:
- factors: bfloat16 [6144, 8, 4096], P('gy', None, 'gz'), may hold values from -0.046875 to 0.046875
- trial_vectors: float32 [64, 8, 4096], P('gx', None, 'gz'), may hold values from -6 to 6
- energy_gap: float32 [8, 4096], P(None, 'gz'), may hold values from 0.5 to 4
Outputs:
- updated_vectors: float32 [64, 8, 4096], P('gx', None, 'gz')
- coupling: float32 [64, 64], P(None, 'gx')
All inputs are finite; a program needn't handle non-finite values.
Results may differ from a plain program's by a relative error of at most 0.02.
Values may be sent and summed in bfloat16 or wider, within the bound.
No kernel may reach another device: no remote copies, remote signals or barrier semaphores. Data moves between devices by JAX's collectives and lax.ppermute only.
A program may use at most 64 MiB of HBM per device.

v0:
```python
import jax
import jax.numpy as jnp
from jax import lax
from jax.sharding import PartitionSpec as P

ITERS = 2


def copy_for_each(array, axis):
    length = lax.axis_size(axis)
    return lax.all_to_all(
        jnp.broadcast_to(array[None], (length, *array.shape)), axis, 0, 0, tiled=True
    )


def over_copies(array, axis):
    everything = copy_for_each(array, axis)
    return jnp.sum(everything, axis=0)


def packed_total(arrays, axis):
    ends = [0]
    for a in arrays:
        ends.append(ends[-1] + a.size)
    so_far = over_copies(jnp.concatenate([a.ravel() for a in arrays]), axis)
    return tuple((so_far[b:e].reshape(a.shape) for a, b, e in zip(arrays, ends, ends[1:])))


def over_copies_2(array, axis):
    return copy_for_each(array, axis).astype(jnp.float32).sum(axis=0)


def padded_to(lines, length):
    spare = -lines.shape[0] % length
    if not spare:
        return lines
    return jnp.concatenate([lines, jnp.zeros((spare, *lines.shape[1:]), lines.dtype)])


def sum_in_two_steps(array, axis):
    lines = array.reshape(-1, *array.shape[1:][-1:])
    padded = padded_to(lines, lax.axis_size(axis))
    own = lax.psum_scatter(padded, axis, scatter_dimension=0, tiled=True)
    whole = lax.all_gather(own, axis, axis=0, tiled=True)
    return whole[: len(lines)].reshape(array.shape)


def in_order(tiles, dim):
    lengths = list(tiles.shape[1:])
    lengths[dim] *= tiles.shape[0]
    return jnp.moveaxis(tiles, 0, dim).reshape(lengths)


def gathered_copies(array, axis, dim):
    return in_order(copy_for_each(array, axis), dim)


def in_blocks(array, dim, length):
    lengths = array.shape
    tiles = array.reshape(*lengths[:dim], length, lengths[dim] // length, *lengths[dim + 1 :])
    return jnp.moveaxis(tiles, dim, 0)


def sum_at_owner(array, axis, dim):
    tiles = in_blocks(array, dim, lax.axis_size(axis))
    arrived = lax.all_to_all(tiles, axis, split_axis=0, concat_axis=0, tiled=True)
    return arrived.astype(jnp.float32).sum(axis=0)


def sum_by_parts(array, axes):
    lines = array.reshape(-1, array.shape[-1])
    padded = padded_to(lines, lax.axis_size(axes))
    whole = gathered_copies(sum_at_owner(padded, axes, 0).astype(jnp.bfloat16), axes, 0)
    return lax.slice_in_dim(whole, 0, len(lines)).reshape(array.shape).astype(jnp.float32)


def solve_subspace(gram_matrix, projected):
    lower_factor = jnp.linalg.cholesky(gram_matrix)
    inner_solve = lax.linalg.triangular_solve(lower_factor, projected, left_side=True, lower=True)
    return lax.linalg.triangular_solve(
        lower_factor, inner_solve, left_side=True, lower=True, transpose_a=True
    )


def correct(own_vectors, gap_share, fock_part):
    highest = lax.Precision.HIGHEST
    everyone = lax.all_gather(own_vectors.astype(jnp.bfloat16), "gx", axis=0, tiled=True).astype(
        own_vectors.dtype
    )
    sigma_own = gap_share[None, :, :] * own_vectors + fock_part
    gram_matrix = jnp.einsum("krn,lrn->kl", everyone, everyone, precision=highest)
    projected = jnp.einsum("lrn,krn->lk", everyone, sigma_own, precision=highest)
    gram_matrix, projected = packed_total((gram_matrix, projected), "gz")
    coupling = solve_subspace(gram_matrix, projected)
    residual = sigma_own - jnp.einsum("lrn,lk->krn", everyone, coupling, precision=highest)
    return (own_vectors - residual / gap_share[None, :, :], coupling)


def per_device(factors, trial_vectors, energy_gap):
    current = trial_vectors
    coupling = None
    for iteration in range(ITERS):
        compact = current.astype(jnp.bfloat16)
        fitted = jnp.einsum("prn,krn->kp", factors, compact, preferred_element_type=jnp.float32)
        fitted = over_copies_2(fitted.astype(jnp.bfloat16), "gz").astype(jnp.float32)
        mixed_fit = jnp.einsum(
            "prn,kln->klrp", factors, compact, preferred_element_type=jnp.float32
        )
        mixed_fit = (
            sum_in_two_steps(mixed_fit.astype(jnp.bfloat16), "gz")
            .astype(jnp.float32)
            .astype(jnp.bfloat16)
        )
        coulomb = jnp.einsum(
            "prn,kp->krn", factors, fitted.astype(jnp.bfloat16), preferred_element_type=jnp.float32
        )
        exchange_part = jnp.einsum(
            "klrp,pln->krn", mixed_fit, factors, preferred_element_type=jnp.float32
        )
        partial_fock = 2.0 * coulomb - exchange_part
        fock_part = sum_by_parts(partial_fock.astype(jnp.bfloat16), "gy")
        current, coupling = correct(current, energy_gap, fock_part)
    return (current, coupling)


def solution(mesh):
    placed = (P("gy", None, "gz"), P("gx", None, "gz"), P(None, "gz"))
    return jax.shard_map(
        per_device,
        mesh=mesh,
        in_specs=placed,
        out_specs=(P("gx", None, "gz"), P(None, "gx")),
        check_vma=False,
    )
```

profile of v0, /device:TPU:2, one launch (start us, length us, event | category | flops | bytes accessed | tf_op | source)
XLA Modules:
  0.0 309.3 jit_solution(6392802762433335574)
XLA Ops:
  8.5 4.2 %fusion.17 = bf16[32,8,8,384]{3,1,2,0:T(8,128)(2,1)S(1)} fusion(bf16[384,8,512]{2,1,0:T(8,128)(2,1)} %param.8, bf16[32,8,512,1]{2,0,1,3:T(8,128)(2,1)S(1)} %bitcast.126), kind=kOutput, calls=%fused_computation.11 | convolution fusion | flops 806092800 | bytes 4980736 | tf_op jit(solution)/shard_map/prn,kln->klrp/dot_general | solution.py:106
  14.3 44.3 %reduce-scatter.3.cloned.1.call-done = bf16[256,384]{1,0:T(8,128)(2,1)} async-done(((bf16[2048,384]{1,0:T(8,128)(2,1)}), bf16[256,384]{1,0:T(8,128)(2,1)}) %reduce-scatter.3.cloned.1.call-update) | async-done | bytes 196624 | tf_op jit(solution)/shard_map/reduce_scatter | solution.py:43
  61.8 15.8 %all_to_all.42 = bf16[8,32,384]{2,1,0:T(8,128)(2,1)} all-to-all(bf16[8,32,384]{2,1,0:T(8,128)(2,1)S(1)} %broadcast_in_dim.12), channel_id=1, replica_groups=mesh['gx'=2,'gy'=16,'gz'=8] {'gz'}, dimensions={0} | all-to-all | bytes 393216 | tf_op jit(solution)/shard_map/all_to_all | solution.py:11
  78.5 13.4 %all-gather.3.cloned.1.call-done = bf16[2048,384]{1,0:T(8,128)(2,1)} async-done(((bf16[256,384]{1,0:T(8,128)(2,1)}), bf16[2048,384]{1,0:T(8,128)(2,1)}) %all-gather.3.cloned.1.call-update) | async-done | bytes 1572880 | tf_op jit(solution)/shard_map/all_gather | solution.py:44
  91.9 3.3 %fusion.20 = f32[32,8,512]{2,1,0:T(8,128)S(1)} fusion(bf16[32,8,8,384]{3,2,1,0:T(8,128)(2,1)} %bitcast.127, bf16[384,8,512]{2,1,0:T(8,128)(2,1)S(1)} %copy-done), kind=kOutput, calls=%fused_computation.12 | convolution fusion | flops 805306368 | bytes 5242880 | tf_op jit(solution)/shard_map/klrp,pln->krn/dot_general | solution.py:117
  97.5 14.4 %all_to_all.43 = bf16[16,16,512]{2,1,0:T(8,128)(2,1)} all-to-all(bf16[16,16,512]{2,1,0:T(8,128)(2,1)S(1)} %bitcast.123), channel_id=1, replica_groups=mesh['gx'=2,'gy'=16,'gz'=8] {'gy'}, dimensions={0} | all-to-all | bytes 524288 | tf_op jit(solution)/shard_map/all_to_all | solution.py:66
  113.6 5.7 %all-to-all-start.2 = ((bf16[16,16,512]{2,1,0:T(8,128)(2,1)}), bf16[16,16,512]{2,1,0:T(8,128)(2,1)}, u32[]{:S(2)}, u32[]{:S(2)}) async-start(bf16[16,16,512]{2,1,0:T(8,128)(2,1)} %broadcast_in_dim.13), calls=%async_computation.3 | async-start | bytes 524288 | tf_op jit(solution)/shard_map/all_to_all | solution.py:11
  119.4 7.3 %all_gather.13 = bf16[64,8,512]{2,0,1:T(8,128)(2,1)S(1)} all-gather(bf16[32,8,512]{2,0,1:T(8,128)(2,1)S(1)} %copy.159), channel_id=1, replica_groups=mesh['gx'=2,'gy'=16,'gz'=8] {'gx'}, dimensions={0}, use_global_device_ids=true | all-gather | bytes 786432 | tf_op jit(solution)/shard_map/all_gather | solution.py:87
  129.7 2.2 convolution_bitcast_fusion.6
  132.2 13.8 %all_to_all.44 = f32[8,1,6144]{2,1,0:T(1,128)S(1)} all-to-all(f32[8,1,6144]{2,1,0:T(1,128)S(1)} %broadcast_in_dim.15), channel_id=1, replica_groups=mesh['gx'=2,'gy'=16,'gz'=8] {'gz'}, dimensions={0} | all-to-all | bytes 393216 | tf_op jit(solution)/shard_map/all_to_all | solution.py:11
  146.4 5.8 %cholesky.44 = f32[64,64]{1,0:T(8,128)S(1)} custom-call(f32[64,64]{1,0:T(8,128)S(1)} %fusion.58), custom_call_target="Cholesky" | custom-call | tf_op jit(solution)/shard_map/jit(cholesky)/cholesky | solution.py:78
  153.5 4.9 %custom-call.11 = f32[1,64,64]{1,2,0:T(8,128)S(1)} custom-call(f32[1,64,64]{2,1,0:T(8,128)S(1)} %fusion.48), custom_call_target="InvertDiagBlocksLowerTriangular" | custom-call | tf_op jit(solution)/shard_map/triangular_solve/custom-call.2 | solution.py:80
  158.9 3.1 fusion.62
  162.0 2.5 fusion.14
  166.0 38.9 %reduce-scatter.5.cloned.1.call-done = bf16[256,384]{1,0:T(8,128)(2,1)} async-done(((bf16[2048,384]{1,0:T(8,128)(2,1)}), bf16[256,384]{1,0:T(8,128)(2,1)}) %reduce-scatter.5.cloned.1.call-update) | async-done | bytes 196624 | tf_op jit(solution)/shard_map/reduce_scatter | solution.py:43
  206.7 15.8 %all_to_all.45 = bf16[8,32,384]{2,1,0:T(8,128)(2,1)S(1)} all-to-all(bf16[8,32,384]{2,1,0:T(8,128)(2,1)S(1)} %broadcast_in_dim.16), channel_id=1, replica_groups=mesh['gx'=2,'gy'=16,'gz'=8] {'gz'}, dimensions={0} | all-to-all | bytes 393216 | tf_op jit(solution)/shard_map/all_to_all | solution.py:11
  222.6 16.8 %all-gather.5.cloned.1.call-done = bf16[2048,384]{1,0:T(8,128)(2,1)} async-done(((bf16[256,384]{1,0:T(8,128)(2,1)}), bf16[2048,384]{1,0:T(8,128)(2,1)}) %all-gather.5.cloned.1.call-update) | async-done | bytes 1572880 | tf_op jit(solution)/shard_map/all_gather | solution.py:44
  239.4 3.3 %fusion.23 = f32[32,8,512]{2,1,0:T(8,128)S(1)} fusion(bf16[32,8,8,384]{3,2,1,0:T(8,128)(2,1)} %bitcast.128, bf16[384,8,512]{2,1,0:T(8,128)(2,1)S(1)} %copy-done), kind=kOutput, calls=%fused_computation.13 | convolution fusion | flops 805306368 | bytes 5242880 | tf_op jit(solution)/shard_map/klrp,pln->krn/dot_general | solution.py:117
  245.0 14.9 %all_to_all.46 = bf16[16,16,512]{2,1,0:T(8,128)(2,1)S(1)} all-to-all(bf16[16,16,512]{2,1,0:T(8,128)(2,1)S(1)} %bitcast.124), channel_id=1, replica_groups=mesh['gx'=2,'gy'=16,'gz'=8] {'gy'}, dimensions={0} | all-to-all | bytes 524288 | tf_op jit(solution)/shard_map/all_to_all | solution.py:66
  260.7 5.3 %all-to-all-start.6 = ((bf16[16,16,512]{2,1,0:T(8,128)(2,1)}), bf16[16,16,512]{2,1,0:T(8,128)(2,1)S(1)}, u32[]{:S(2)}, u32[]{:S(2)}) async-start(bf16[16,16,512]{2,1,0:T(8,128)(2,1)} %broadcast_in_dim.17), calls=%async_computation.8 | async-start | bytes 524288 | tf_op jit(solution)/shard_map/all_to_all | solution.py:11
  266.0 7.4 %all_gather.15 = bf16[64,8,512]{2,0,1:T(8,128)(2,1)S(1)} all-gather(bf16[32,8,512]{2,0,1:T(8,128)(2,1)S(1)} %copy-done.5), channel_id=1, replica_groups=mesh['gx'=2,'gy'=16,'gz'=8] {'gx'}, dimensions={0}, use_global_device_ids=true | all-gather | bytes 786432 | tf_op jit(solution)/shard_map/all_gather | solution.py:87
  275.0 13.2 %all_to_all.47 = f32[8,1,6144]{2,1,0:T(1,128)S(1)} all-to-all(f32[8,1,6144]{2,1,0:T(1,128)S(1)} %broadcast_in_dim.18), channel_id=1, replica_groups=mesh['gx'=2,'gy'=16,'gz'=8] {'gz'}, dimensions={0} | all-to-all | bytes 393216 | tf_op jit(solution)/shard_map/all_to_all | solution.py:11
  288.5 5.8 %cholesky.55 = f32[64,64]{1,0:T(8,128)S(1)} custom-call(f32[64,64]{1,0:T(8,128)S(1)} %fusion.54), custom_call_target="Cholesky" | custom-call | tf_op jit(solution)/shard_map/jit(cholesky)/cholesky | solution.py:78
  295.7 4.9 %custom-call.13 = f32[1,64,64]{1,2,0:T(8,128)S(1)} custom-call(f32[1,64,64]{2,1,0:T(8,128)S(1)} %fusion.49), custom_call_target="InvertDiagBlocksLowerTriangular" | custom-call | tf_op jit(solution)/shard_map/triangular_solve/custom-call.2 | solution.py:80
  (84 shorter events, 28.0 us)
Async XLA Ops:
  7.2 51.4 %reduce-scatter.3.cloned.1.call-start = ((), (), s32[]{:S(2)}) async-start(), calls=%async_computation.10 | async-start | bytes 1769472 | tf_op jit(solution)/shard_map/reduce_scatter | solution.py:43
  12.8 47.2 %copy-start = (bf16[384,8,512]{2,1,0:T(8,128)(2,1)S(1)}, bf16[384,8,512]{2,1,0:T(8,128)(2,1)}, u32[]{:S(2)}) copy-start(bf16[384,8,512]{2,1,0:T(8,128)(2,1)} %param.8) | copy-start | bytes 9437188
  14.3 77.6 %all-gather.3.cloned.1.call-start = ((), (), s32[]{:S(2)}) async-start(), calls=%async_computation.11 | async-start | bytes 1769472 | tf_op jit(solution)/shard_map/all_gather | solution.py:44
  97.3 32.4 %copy-start.6 = (f32[8,512]{1,0:T(8,128)S(1)}, f32[8,512]{1,0:T(8,128)}, u32[]{:S(2)}) copy-start(f32[8,512]{1,0:T(8,128)} %param.10) | copy-start | bytes 49156
  113.6 14.2 %all-to-all-start.2 = ((bf16[16,16,512]{2,1,0:T(8,128)(2,1)}), bf16[16,16,512]{2,1,0:T(8,128)(2,1)}, u32[]{:S(2)}, u32[]{:S(2)}) async-start(bf16[16,16,512]{2,1,0:T(8,128)(2,1)} %broadcast_in_dim.13), calls=%async_computation.3 | async-start | bytes 524288 | tf_op jit(solution)/shard_map/all_to_all | solution.py:11
  119.3 85.5 %reduce-scatter.5.cloned.1.call-start = ((), (), s32[]{:S(2)}) async-start(), calls=%async_computation.12 | async-start | bytes 1769472 | tf_op jit(solution)/shard_map/reduce_scatter | solution.py:43
  126.7 0.8 copy-start.1
  128.9 0.8 copy-start.2
  162.0 42.9 %copy-start.4 = (bf16[32,8,512]{2,0,1:T(8,128)(2,1)}, bf16[32,8,512]{2,0,1:T(8,128)(2,1)S(1)}, u32[]{:S(2)}) copy-start(bf16[32,8,512]{2,0,1:T(8,128)(2,1)S(1)} %get-tuple-element.13) | copy-start | bytes 786436
  165.9 73.4 %all-gather.5.cloned.1.call-start = ((), (), s32[]{:S(2)}) async-start(), calls=%async_computation.13 | async-start | bytes 1769472 | tf_op jit(solution)/shard_map/all_gather | solution.py:44
  242.7 23.3 %copy-start.5 = (bf16[32,8,512]{2,0,1:T(8,128)(2,1)S(1)}, bf16[32,8,512]{2,0,1:T(8,128)(2,1)}, u32[]{:S(2)}) copy-start(bf16[32,8,512]{2,0,1:T(8,128)(2,1)} %copy-done.4) | copy-start | bytes 786436
  244.8 29.1 %copy-start.3 = (f32[32,8,512]{2,0,1:T(8,128)S(1)}, f32[32,8,512]{2,0,1:T(8,128)}, u32[]{:S(2)}) copy-start(f32[32,8,512]{2,0,1:T(8,128)} %get-tuple-element.14) | copy-start | bytes 1572868
  260.7 13.1 %all-to-all-start.6 = ((bf16[16,16,512]{2,1,0:T(8,128)(2,1)}), bf16[16,16,512]{2,1,0:T(8,128)(2,1)S(1)}, u32[]{:S(2)}, u32[]{:S(2)}) async-start(bf16[16,16,512]{2,1,0:T(8,128)(2,1)} %broadcast_in_dim.17), calls=%async_computation.8 | async-start | bytes 524288 | tf_op jit(solution)/shard_map/all_to_all | solution.py:11
  301.1 1.7 copy-start.7
Sparse Core Ops, SparseCore 0:
  14.4 44.1 reduce-scatter.2
  60.4 31.4 all-gather.2
  166.1 38.7 reduce-scatter.4
  206.6 32.7 all-gather.4
where the time goes:
time: 310 us; the launch traced here: 309 us
  waiting for transfers between devices  113 us (36%)
  blocking collectives  103 us (33%)
  matrix products  29.2 us (9%)
  other arithmetic  27.6 us (9%)
  between operations  14.1 us (5%)
  starting transfers between devices  11.2 us (4%)
  local copies, waits for them, and re-layouts  11.1 us (4%)
    reduce_scatter x2, waiting for transfers between devices, sum_in_two_steps(): own = lax.psum_scatter(padded, axis, scatter_dimension=0, tiled=True)  83.2 us
    all_to_all x4, blocking collectives, copy_for_each(): lax.all_to_all(jnp.broadcast_to(array[None], (length, *array.shape)), axi...  58.6 us
    all_gather x2, waiting for transfers between devices, sum_in_two_steps(): whole = lax.all_gather(own, axis, axis=0, tiled=True)  30.2 us
    all_to_all x2, blocking collectives, sum_at_owner(): lax.all_to_all(tiles, axis, split_axis=0, concat_axis=0, tiled=True)  29.4 us
    all_gather x2, blocking collectives, correct(): lax.all_gather(own_vectors.astype(jnp.bfloat16), 'gx', axis=0, tiled=True)  14.7 us
    another operation x6, other arithmetic, solve_subspace(): lower_factor = jnp.linalg.cholesky(gram_matrix)  13 us
    another operation x4, other arithmetic, solve_subspace(): lax.linalg.triangular_solve(lower_factor, inner_solve, left_side=True, lo...  11.1 us
    all_to_all x2, starting transfers between devices, copy_for_each(): lax.all_to_all(jnp.broadcast_to(array[None], (length, *array.shape)), axi...  11.1 us
  transfers between devices with their start and end apart: 6, of which 4 were waited for; matrix products, arithmetic and copies ran while one was open for 2% of the time, Pallas kernels for 0%

commit v1 on v0

--- a/solution.py
+++ b/solution.py
@@ -41,7 +41,15 @@
     lines = array.reshape(-1, *array.shape[1:][-1:])
     padded = padded_to(lines, lax.axis_size(axis))
     own = lax.psum_scatter(padded, axis, scatter_dimension=0, tiled=True)
-    whole = lax.all_gather(own, axis, axis=0, tiled=True)
+    whole = jnp.concatenate(
+        lax.all_to_all(
+            jnp.stack(lax.psum(1, axis_name=axis) * [own], axis=0),
+            axis_name=axis,
+            split_axis=0,
+            concat_axis=0,
+        ),
+        axis=0,
+    )
     return whole[: len(lines)].reshape(array.shape)
 
 

time: 310 us -> 338 us (1.090)
  waiting for transfers between devices: 113 us -> 126 us
  starting transfers between devices: 11.2 us -> 21.5 us
  local copies, waits for them, and re-layouts: 11.1 us -> 15.6 us
    all_to_all x0 -> x2, waiting for transfers between devices: none -> 80.5 us  [sum_in_two_steps(): lax.all_to_all(jnp.stack(lax.psum(1, axis_name=axis) * [own], axis=0), ax...]
    reduce_scatter x2, waiting for transfers between devices: 83.2 us -> 45.6 us  [sum_in_two_steps(): own = lax.psum_scatter(padded, axis, scatter_dimension=0, tiled=True)]
    all_gather x2 -> x0, waiting for transfers between devices: 30.2 us -> none  [sum_in_two_steps(): whole = lax.all_gather(own, axis, axis=0, tiled=True)]
    all_to_all x0 -> x2, starting transfers between devices: none -> 10.6 us  [sum_in_two_steps(): lax.all_to_all(jnp.stack(lax.psum(1, axis_name=axis) * [own], axis=0), ax...]
    another operation x0 -> x2, local copies, waits for them, and re-layouts: none -> 4.44 us  [sum_in_two_steps(): jnp.stack(lax.psum(1, axis_name=axis) * [own], axis=0)]
where the time goes in v1:
time: 338 us; the launch traced here: 337 us
  waiting for transfers between devices  126 us (37%)
  blocking collectives  102 us (30%)
  matrix products  29.2 us (9%)
  other arithmetic  27.6 us (8%)
  starting transfers between devices  21.5 us (6%)
  local copies, waits for them, and re-layouts  15.6 us (5%)
  between operations  14.4 us (4%)
    all_to_all x2, waiting for transfers between devices, sum_in_two_steps(): lax.all_to_all(jnp.stack(lax.psum(1, axis_name=axis) * [own], axis=0), ax...  80.5 us
    all_to_all x4, blocking collectives, copy_for_each(): lax.all_to_all(jnp.broadcast_to(array[None], (length, *array.shape)), axi...  60.1 us
    reduce_scatter x2, waiting for transfers between devices, sum_in_two_steps(): own = lax.psum_scatter(padded, axis, scatter_dimension=0, tiled=True)  45.6 us
    all_to_all x2, blocking collectives, sum_at_owner(): lax.all_to_all(tiles, axis, split_axis=0, concat_axis=0, tiled=True)  28 us
    all_gather x2, blocking collectives, correct(): lax.all_gather(own_vectors.astype(jnp.bfloat16), 'gx', axis=0, tiled=True)  14.1 us
    another operation x6, other arithmetic, solve_subspace(): lower_factor = jnp.linalg.cholesky(gram_matrix)  13 us
    another operation x4, other arithmetic, solve_subspace(): lax.linalg.triangular_solve(lower_factor, inner_solve, left_side=True, lo...  11.1 us
    all_to_all x2, starting transfers between devices, copy_for_each(): lax.all_to_all(jnp.broadcast_to(array[None], (length, *array.shape)), axi...  10.8 us
  transfers between devices with their start and end apart: 6, of which 4 were waited for; matrix products, arithmetic and copies ran while one was open for 2% of the time, Pallas kernels for 0%

profile of v1, /device:TPU:2, one launch (start us, length us, event | category | flops | bytes accessed | tf_op | source)
XLA Modules:
  0.0 336.6 jit_solution(1750152803566594411)
XLA Ops:
  8.5 4.2 %fusion.17 = bf16[32,8,8,384]{3,1,2,0:T(8,128)(2,1)S(1)} fusion(bf16[384,8,512]{2,1,0:T(8,128)(2,1)} %param.8, bf16[32,8,512,1]{2,0,1,3:T(8,128)(2,1)S(1)} %bitcast.126), kind=kOutput, calls=%fused_computation.11 | convolution fusion | flops 806092800 | bytes 4980736 | tf_op jit(solution)/shard_map/prn,kln->klrp/dot_general | solution.py:114
  17.5 20.0 %all_to_all.52 = bf16[8,32,384]{2,1,0:T(8,128)(2,1)} all-to-all(bf16[8,32,384]{2,1,0:T(8,128)(2,1)S(1)} %broadcast_in_dim.12), channel_id=1, replica_groups=mesh['gx'=2,'gy'=16,'gz'=8] {'gz'}, dimensions={0} | all-to-all | bytes 393216 | tf_op jit(solution)/shard_map/all_to_all | solution.py:11
  37.4 21.7 %reduce-scatter.3.cloned.1.call-done = bf16[256,384]{1,0:T(8,128)(2,1)} async-done(((bf16[2048,384]{1,0:T(8,128)(2,1)}), bf16[256,384]{1,0:T(8,128)(2,1)}) %reduce-scatter.3.cloned.1.call-update) | async-done | bytes 196624 | tf_op jit(solution)/shard_map/reduce_scatter | solution.py:43
  61.3 6.1 %all-to-all-start.1 = ((bf16[8,256,384]{2,1,0:T(8,128)(2,1)}), bf16[8,256,384]{2,1,0:T(8,128)(2,1)}, u32[]{:S(2)}, u32[]{:S(2)}) async-start(bf16[8,256,384]{2,1,0:T(8,128)(2,1)} %stack.4), calls=%async_computation.2 | async-start | bytes 3145728 | tf_op jit(solution)/shard_map/all_to_all | solution.py:45
  68.4 40.0 %all-to-all-done.1 = bf16[8,256,384]{2,1,0:T(8,128)(2,1)} async-done(((bf16[8,256,384]{2,1,0:T(8,128)(2,1)}), bf16[8,256,384]{2,1,0:T(8,128)(2,1)}, u32[]{:S(2)}, u32[]{:S(2)}) %all-to-all-start.1) | async-done | bytes 1572896 | tf_op jit(solution)/shard_map/all_to_all | solution.py:45
  108.3 3.3 fusion.20
  113.9 13.8 %all_to_all.53 = bf16[16,16,512]{2,1,0:T(8,128)(2,1)} all-to-all(bf16[16,16,512]{2,1,0:T(8,128)(2,1)S(1)} %bitcast.123), channel_id=1, replica_groups=mesh['gx'=2,'gy'=16,'gz'=8] {'gy'}, dimensions={0} | all-to-all | bytes 524288 | tf_op jit(solution)/shard_map/all_to_all | solution.py:74
  129.5 5.7 %all-to-all-start.3 = ((bf16[16,16,512]{2,1,0:T(8,128)(2,1)}), bf16[16,16,512]{2,1,0:T(8,128)(2,1)}, u32[]{:S(2)}, u32[]{:S(2)}) async-start(bf16[16,16,512]{2,1,0:T(8,128)(2,1)} %broadcast_in_dim.13), calls=%async_computation.4 | async-start | bytes 524288 | tf_op jit(solution)/shard_map/all_to_all | solution.py:11
  135.2 7.0 %all_gather.6 = bf16[64,8,512]{2,0,1:T(8,128)(2,1)S(1)} all-gather(bf16[32,8,512]{2,0,1:T(8,128)(2,1)S(1)} %copy.159), channel_id=1, replica_groups=mesh['gx'=2,'gy'=16,'gz'=8] {'gx'}, dimensions={0}, use_global_device_ids=true | all-gather | bytes 786432 | tf_op jit(solution)/shard_map/all_gather | solution.py:95
  147.8 13.3 %all_to_all.54 = f32[8,1,6144]{2,1,0:T(1,128)S(1)} all-to-all(f32[8,1,6144]{2,1,0:T(1,128)S(1)} %broadcast_in_dim.15), channel_id=1, replica_groups=mesh['gx'=2,'gy'=16,'gz'=8] {'gz'}, dimensions={0} | all-to-all | bytes 393216 | tf_op jit(solution)/shard_map/all_to_all | solution.py:11
  161.4 5.8 %cholesky.44 = f32[64,64]{1,0:T(8,128)S(1)} custom-call(f32[64,64]{1,0:T(8,128)S(1)} %fusion.58), custom_call_target="Cholesky" | custom-call | tf_op jit(solution)/shard_map/jit(cholesky)/cholesky | solution.py:86
  168.6 4.9 %custom-call.11 = f32[1,64,64]{1,2,0:T(8,128)S(1)} custom-call(f32[1,64,64]{2,1,0:T(8,128)S(1)} %fusion.48), custom_call_target="InvertDiagBlocksLowerTriangular" | custom-call | tf_op jit(solution)/shard_map/triangular_solve/custom-call.2 | solution.py:88
  174.0 3.0 fusion.62
  182.8 13.1 %all_to_all.55 = bf16[8,32,384]{2,1,0:T(8,128)(2,1)S(1)} all-to-all(bf16[8,32,384]{2,1,0:T(8,128)(2,1)S(1)} %broadcast_in_dim.16), channel_id=1, replica_groups=mesh['gx'=2,'gy'=16,'gz'=8] {'gz'}, dimensions={0} | all-to-all | bytes 393216 | tf_op jit(solution)/shard_map/all_to_all | solution.py:11
  195.9 23.9 %reduce-scatter.5.cloned.1.call-done = bf16[256,384]{1,0:T(8,128)(2,1)} async-done(((bf16[2048,384]{1,0:T(8,128)(2,1)}), bf16[256,384]{1,0:T(8,128)(2,1)}) %reduce-scatter.5.cloned.1.call-update) | async-done | bytes 196624 | tf_op jit(solution)/shard_map/reduce_scatter | solution.py:43
  222.0 4.5 %all-to-all-start.6 = ((bf16[8,256,384]{2,1,0:T(8,128)(2,1)}), bf16[8,256,384]{2,1,0:T(8,128)(2,1)}, u32[]{:S(2)}, u32[]{:S(2)}) async-start(bf16[8,256,384]{2,1,0:T(8,128)(2,1)} %stack.5), calls=%async_computation.8 | async-start | bytes 3145728 | tf_op jit(solution)/shard_map/all_to_all | solution.py:45
  226.6 40.6 %all-to-all-done.6 = bf16[8,256,384]{2,1,0:T(8,128)(2,1)} async-done(((bf16[8,256,384]{2,1,0:T(8,128)(2,1)}), bf16[8,256,384]{2,1,0:T(8,128)(2,1)}, u32[]{:S(2)}, u32[]{:S(2)}) %all-to-all-start.6) | async-done | bytes 1572896 | tf_op jit(solution)/shard_map/all_to_all | solution.py:45
  267.1 3.3 fusion.23
  272.7 14.2 %all_to_all.56 = bf16[16,16,512]{2,1,0:T(8,128)(2,1)S(1)} all-to-all(bf16[16,16,512]{2,1,0:T(8,128)(2,1)S(1)} %bitcast.124), channel_id=1, replica_groups=mesh['gx'=2,'gy'=16,'gz'=8] {'gy'}, dimensions={0} | all-to-all | bytes 524288 | tf_op jit(solution)/shard_map/all_to_all | solution.py:74
  287.7 5.1 %all-to-all-start.8 = ((bf16[16,16,512]{2,1,0:T(8,128)(2,1)}), bf16[16,16,512]{2,1,0:T(8,128)(2,1)S(1)}, u32[]{:S(2)}, u32[]{:S(2)}) async-start(bf16[16,16,512]{2,1,0:T(8,128)(2,1)} %broadcast_in_dim.17), calls=%async_computation.10 | async-start | bytes 524288 | tf_op jit(solution)/shard_map/all_to_all | solution.py:11
  292.8 7.0 %all_gather.7 = bf16[64,8,512]{2,0,1:T(8,128)(2,1)S(1)} all-gather(bf16[32,8,512]{2,0,1:T(8,128)(2,1)S(1)} %copy-done.5), channel_id=1, replica_groups=mesh['gx'=2,'gy'=16,'gz'=8] {'gx'}, dimensions={0}, use_global_device_ids=true | all-gather | bytes 786432 | tf_op jit(solution)/shard_map/all_gather | solution.py:95
  301.4 13.7 %all_to_all.57 = f32[8,1,6144]{2,1,0:T(1,128)S(1)} all-to-all(f32[8,1,6144]{2,1,0:T(1,128)S(1)} %broadcast_in_dim.18), channel_id=1, replica_groups=mesh['gx'=2,'gy'=16,'gz'=8] {'gz'}, dimensions={0} | all-to-all | bytes 393216 | tf_op jit(solution)/shard_map/all_to_all | solution.py:11
  315.4 5.8 %cholesky.55 = f32[64,64]{1,0:T(8,128)S(1)} custom-call(f32[64,64]{1,0:T(8,128)S(1)} %fusion.54), custom_call_target="Cholesky" | custom-call | tf_op jit(solution)/shard_map/jit(cholesky)/cholesky | solution.py:86
  322.6 4.9 %custom-call.13 = f32[1,64,64]{1,2,0:T(8,128)S(1)} custom-call(f32[1,64,64]{2,1,0:T(8,128)S(1)} %fusion.49), custom_call_target="InvertDiagBlocksLowerTriangular" | custom-call | tf_op jit(solution)/shard_map/triangular_solve/custom-call.2 | solution.py:88
  (84 shorter events, 37.1 us)
Async XLA Ops:
  7.2 52.0 %reduce-scatter.3.cloned.1.call-start = ((), (), s32[]{:S(2)}) async-start(), calls=%async_computation.12 | async-start | bytes 1769472 | tf_op jit(solution)/shard_map/reduce_scatter | solution.py:43
  12.8 2.9 copy-start
  61.3 47.0 %all-to-all-start.1 = ((bf16[8,256,384]{2,1,0:T(8,128)(2,1)}), bf16[8,256,384]{2,1,0:T(8,128)(2,1)}, u32[]{:S(2)}, u32[]{:S(2)}) async-start(bf16[8,256,384]{2,1,0:T(8,128)(2,1)} %stack.4), calls=%async_computation.2 | async-start | bytes 3145728 | tf_op jit(solution)/shard_map/all_to_all | solution.py:45
  113.8 31.5 %copy-start.6 = (f32[8,512]{1,0:T(8,128)S(1)}, f32[8,512]{1,0:T(8,128)}, u32[]{:S(2)}) copy-start(f32[8,512]{1,0:T(8,128)} %param.10) | copy-start | bytes 49156
  129.5 13.9 %all-to-all-start.3 = ((bf16[16,16,512]{2,1,0:T(8,128)(2,1)}), bf16[16,16,512]{2,1,0:T(8,128)(2,1)}, u32[]{:S(2)}, u32[]{:S(2)}) async-start(bf16[16,16,512]{2,1,0:T(8,128)(2,1)} %broadcast_in_dim.13), calls=%async_computation.4 | async-start | bytes 524288 | tf_op jit(solution)/shard_map/all_to_all | solution.py:11
  135.2 84.6 %reduce-scatter.5.cloned.1.call-start = ((), (), s32[]{:S(2)}) async-start(), calls=%async_computation.13 | async-start | bytes 1769472 | tf_op jit(solution)/shard_map/reduce_scatter | solution.py:43
  142.3 0.8 copy-start.1
  144.4 0.8 copy-start.2
  177.0 3.9 %copy-start.4 = (bf16[32,8,512]{2,0,1:T(8,128)(2,1)}, bf16[32,8,512]{2,0,1:T(8,128)(2,1)S(1)}, u32[]{:S(2)}) copy-start(bf16[32,8,512]{2,0,1:T(8,128)(2,1)S(1)} %get-tuple-element.13) | copy-start | bytes 786436
  222.0 45.1 %all-to-all-start.6 = ((bf16[8,256,384]{2,1,0:T(8,128)(2,1)}), bf16[8,256,384]{2,1,0:T(8,128)(2,1)}, u32[]{:S(2)}, u32[]{:S(2)}) async-start(bf16[8,256,384]{2,1,0:T(8,128)(2,1)} %stack.5), calls=%async_computation.8 | async-start | bytes 3145728 | tf_op jit(solution)/shard_map/all_to_all | solution.py:45
  270.4 22.4 %copy-start.5 = (bf16[32,8,512]{2,0,1:T(8,128)(2,1)S(1)}, bf16[32,8,512]{2,0,1:T(8,128)(2,1)}, u32[]{:S(2)}) copy-start(bf16[32,8,512]{2,0,1:T(8,128)(2,1)} %copy-done.4) | copy-start | bytes 786436
  272.6 27.7 %copy-start.3 = (f32[32,8,512]{2,0,1:T(8,128)S(1)}, f32[32,8,512]{2,0,1:T(8,128)}, u32[]{:S(2)}) copy-start(f32[32,8,512]{2,0,1:T(8,128)} %get-tuple-element.14) | copy-start | bytes 1572868
  287.7 12.5 %all-to-all-start.8 = ((bf16[16,16,512]{2,1,0:T(8,128)(2,1)}), bf16[16,16,512]{2,1,0:T(8,128)(2,1)S(1)}, u32[]{:S(2)}, u32[]{:S(2)}) async-start(bf16[16,16,512]{2,1,0:T(8,128)(2,1)} %broadcast_in_dim.17), calls=%async_computation.10 | async-start | bytes 524288 | tf_op jit(solution)/shard_map/all_to_all | solution.py:11
  328.0 1.7 copy-start.7
Sparse Core Ops, SparseCore 0:
  14.4 44.6 reduce-scatter.2
  181.1 38.6 reduce-scatter.4
